TPU v7x, 32 devices: a whole 2x2x4 slice. The times are simulated.
32 devices in a mesh: slab: 2 (over core), py: 4 (over z), pz: 4 (over y, x).
Axes of the slice: x: 2, y: 2, z: 4, core: 2. Of those that a mesh axis runs over, the one named last changes fastest.
Arguments:
- start_vector: float32 [32, 128, 256], P('pz', 'py', 'slab'), may hold values from -6 to 6
- potential: float32 [32, 128, 256], P('pz', 'py', 'slab'), may hold values from 0.5 to 4
Outputs:
- krylov_basis: float32 [6, 32, 128, 256], P(None, 'pz', 'py', 'slab')
- tridiagonal: float32 [2, 5], replicated
All inputs are finite; a program needn't handle non-finite values.
Results may differ from a plain program's by a relative error of at most 0.00012.
Values sent between devices are 32-bit elements; how exact they have to be, the bound alone decides.
A program may use at most 64 MiB of HBM per device.

v0:
```python
import jax
import jax.numpy as jnp
from jax import lax
from jax.sharding import PartitionSpec as P

ITERS = 5
EPSILON = 1e-06


def with_halo(block, sides, width):
    for axis, dim in sides:
        count = lax.axis_size(axis)
        forward = [(i, i + 1) for i in range(count - 1)]
        backward = [(target, source) for source, target in forward]
        low = lax.ppermute(
            lax.slice_in_dim(block, block.shape[dim] - width, None, axis=dim), axis, forward
        )
        high = lax.ppermute(lax.slice_in_dim(block, 0, width, axis=dim), axis, backward)
        block = jnp.concatenate([low, block, high], axis=dim)
    return block


def apply_hamiltonian(field, potential):
    padded = with_halo(field, (("slab", 2), ("py", 1), ("pz", 0)), 1)
    beside = padded[2:, 1:-1, 1:-1] + padded[:-2, 1:-1, 1:-1]
    beside = beside + padded[1:-1, 2:, 1:-1] + padded[1:-1, :-2, 1:-1]
    beside = beside + padded[1:-1, 1:-1, 2:] + padded[1:-1, 1:-1, :-2]
    return (6.0 + potential) * field - beside


def reduce_all(partials):
    inner = lax.psum(partials, "pz")
    return lax.psum(inner, ("slab", "py"))


def project(active, image):
    return jnp.einsum("kzyx,zyx->k", active, image, precision=lax.Precision.HIGHEST)


def remove(image, coeffs, active):
    return image - jnp.einsum("k,kzyx->zyx", coeffs, active, precision=lax.Precision.HIGHEST)


def shards(start_vector, potential):
    cell_count = (
        start_vector.size * lax.axis_size("slab") * lax.axis_size("py") * lax.axis_size("pz")
    )
    per_cell = jnp.float32(1.0 / cell_count)
    start_norm = reduce_all(jnp.sum(start_vector * start_vector).reshape(1))[0] * per_cell
    vectors = [start_vector / jnp.sqrt(start_norm + EPSILON)]
    alphas = []
    beta_list = []
    for iteration in range(ITERS):
        image = apply_hamiltonian(vectors[-1], potential)
        active = jnp.stack(vectors)
        first_coeff = reduce_all(project(active, image)) * per_cell
        image = remove(image, first_coeff, active)
        local_second = project(active, image)
        summed = (
            reduce_all(jnp.concatenate([local_second, jnp.sum(image * image).reshape(1)]))
            * per_cell
        )
        second_coeff = summed[:-1]
        image = remove(image, second_coeff, active)
        square_mean = summed[-1] - jnp.sum(second_coeff * second_coeff)
        beta_value = jnp.sqrt(square_mean + EPSILON)
        alphas.append(first_coeff[iteration] + second_coeff[iteration])
        beta_list.append(beta_value)
        vectors.append(image / beta_value)
    return (jnp.stack(vectors), jnp.stack([jnp.stack(alphas), jnp.stack(beta_list)]))


def solution(mesh):
    in_specs = (P("pz", "py", "slab"), P("pz", "py", "slab"))
    out_specs = (P(None, "pz", "py", "slab"), P())
    return jax.shard_map(shards, mesh=mesh, in_specs=in_specs, out_specs=out_specs, check_vma=False)
```

profile of v0, /device:TPU:0, one launch (start us, length us, event | category | flops | bytes accessed | tf_op | source)
XLA Modules:
  0.0 438.7 jit_solution(16922644488798986109)
XLA Ops:
  2.2 12.0 %psum.154 = f32[1]{0:T(128)} all-reduce(f32[1]{0:T(128)} %bitcast.4), channel_id=1, replica_groups=mesh['slab'=2,'py'=4,'pz'=4] {'pz'}, use_global_device_ids=true, to_apply=%region_1.0 | all-reduce | flops 1 | bytes 8 | tf_op jit(solution)/shard_map/psum | solution.py:32
  14.2 16.0 %psum.155 = f32[1]{0:T(128)} all-reduce(f32[1]{0:T(128)} %psum.154), channel_id=1, replica_groups=mesh['slab'=2,'py'=4,'pz'=4] {'slab','py'}, use_global_device_ids=true, to_apply=%region_2.0 | all-reduce | flops 1 | bytes 8 | tf_op jit(solution)/shard_map/psum | solution.py:33
  41.1 4.2 collective-permute-done.3
  48.7 4.6 %collective-permute-done.4 = f32[1,34,130]{2,1,0:T(8,128)S(1)} collective-permute-done((f32[1,34,130]{2,1,0:T(8,128)S(1)}, f32[1,34,130]{2,1,0:T(8,128)S(1)}, u32[]{:S(2)}, u32[]{:S(2)}) %collective-permute-start.4) | collective-permute-done | bytes 17712 | tf_op jit(solution)/shard_map/ppermute | solution.py:18
  54.2 11.0 %psum.156 = f32[1]{0:T(128)} all-reduce(f32[1]{0:T(128)} %bitcast.7), channel_id=1, replica_groups=mesh['slab'=2,'py'=4,'pz'=4] {'pz'}, use_global_device_ids=true, to_apply=%region_3.0 | all-reduce | flops 1 | bytes 8 | tf_op jit(solution)/shard_map/psum | solution.py:32
  65.2 14.7 %psum.157 = f32[1]{0:T(128)} all-reduce(f32[1]{0:T(128)} %psum.156), channel_id=1, replica_groups=mesh['slab'=2,'py'=4,'pz'=4] {'slab','py'}, use_global_device_ids=true, to_apply=%region_4.0 | all-reduce | flops 1 | bytes 8 | tf_op jit(solution)/shard_map/psum | solution.py:33
  83.3 7.4 %psum.158 = f32[2]{0:T(128)S(1)} all-reduce(f32[2]{0:T(128)S(1)} %pad_maximum_fusion.134), channel_id=1, replica_groups=mesh['slab'=2,'py'=4,'pz'=4] {'pz'}, use_global_device_ids=true, to_apply=%region_6.0 | all-reduce | flops 2 | bytes 16 | tf_op jit(solution)/shard_map/psum | solution.py:32
  90.7 15.6 %psum.159 = f32[2]{0:T(128)S(1)} all-reduce(f32[2]{0:T(128)S(1)} %psum.158), channel_id=1, replica_groups=mesh['slab'=2,'py'=4,'pz'=4] {'slab','py'}, use_global_device_ids=true, to_apply=%region_7.0 | all-reduce | flops 2 | bytes 16 | tf_op jit(solution)/shard_map/psum | solution.py:33
  118.1 4.2 collective-permute-done.9
  122.4 3.9 collective-permute-start.11
  128.0 4.2 collective-permute-done.10
  135.0 9.3 %psum.160 = f32[2]{0:T(128)S(1)} all-reduce(f32[2]{0:T(128)S(1)} %convolution_bitcast_fusion.5), channel_id=1, replica_groups=mesh['slab'=2,'py'=4,'pz'=4] {'pz'}, use_global_device_ids=true, to_apply=%region_8.0 | all-reduce | flops 2 | bytes 16 | tf_op jit(solution)/shard_map/psum | solution.py:32
  144.2 14.4 %psum.161 = f32[2]{0:T(128)S(1)} all-reduce(f32[2]{0:T(128)S(1)} %psum.160), channel_id=1, replica_groups=mesh['slab'=2,'py'=4,'pz'=4] {'slab','py'}, use_global_device_ids=true, to_apply=%region_9.0 | all-reduce | flops 2 | bytes 16 | tf_op jit(solution)/shard_map/psum | solution.py:33
  163.3 8.5 %psum.162 = f32[3]{0:T(128)S(1)} all-reduce(f32[3]{0:T(128)S(1)} %pad_maximum_fusion.135), channel_id=1, replica_groups=mesh['slab'=2,'py'=4,'pz'=4] {'pz'}, use_global_device_ids=true, to_apply=%region_11.0 | all-reduce | flops 3 | bytes 24 | tf_op jit(solution)/shard_map/psum | solution.py:32
  171.8 15.2 %psum.163 = f32[3]{0:T(128)S(1)} all-reduce(f32[3]{0:T(128)S(1)} %psum.162), channel_id=1, replica_groups=mesh['slab'=2,'py'=4,'pz'=4] {'slab','py'}, use_global_device_ids=true, to_apply=%region_12.0 | all-reduce | flops 3 | bytes 24 | tf_op jit(solution)/shard_map/psum | solution.py:33
  199.4 4.2 collective-permute-done.15
  208.2 4.2 collective-permute-done.16
  215.2 9.4 %psum.164 = f32[3]{0:T(128)S(1)} all-reduce(f32[3]{0:T(128)S(1)} %convolution_bitcast_fusion.3), channel_id=1, replica_groups=mesh['slab'=2,'py'=4,'pz'=4] {'pz'}, use_global_device_ids=true, to_apply=%region_14.0 | all-reduce | flops 3 | bytes 24 | tf_op jit(solution)/shard_map/psum | solution.py:32
  224.6 14.2 %psum.165 = f32[3]{0:T(128)S(1)} all-reduce(f32[3]{0:T(128)S(1)} %psum.164), channel_id=1, replica_groups=mesh['slab'=2,'py'=4,'pz'=4] {'slab','py'}, use_global_device_ids=true, to_apply=%region_15.0 | all-reduce | flops 3 | bytes 24 | tf_op jit(solution)/shard_map/psum | solution.py:33
  243.8 8.3 %psum.166 = f32[4]{0:T(128)S(1)} all-reduce(f32[4]{0:T(128)S(1)} %pad_maximum_fusion.136), channel_id=1, replica_groups=mesh['slab'=2,'py'=4,'pz'=4] {'pz'}, use_global_device_ids=true, to_apply=%region_17.0 | all-reduce | flops 4 | bytes 32 | tf_op jit(solution)/shard_map/psum | solution.py:32
  252.1 15.6 %psum.167 = f32[4]{0:T(128)S(1)} all-reduce(f32[4]{0:T(128)S(1)} %psum.166), channel_id=1, replica_groups=mesh['slab'=2,'py'=4,'pz'=4] {'slab','py'}, use_global_device_ids=true, to_apply=%region_18.0 | all-reduce | flops 4 | bytes 32 | tf_op jit(solution)/shard_map/psum | solution.py:33
  279.8 4.2 collective-permute-done.21
  288.8 4.2 collective-permute-done.22
  295.9 9.3 %psum.168 = f32[4]{0:T(128)S(1)} all-reduce(f32[4]{0:T(128)S(1)} %convolution_bitcast_fusion.1), channel_id=1, replica_groups=mesh['slab'=2,'py'=4,'pz'=4] {'pz'}, use_global_device_ids=true, to_apply=%region_20.0 | all-reduce | flops 4 | bytes 32 | tf_op jit(solution)/shard_map/psum | solution.py:32
  305.2 14.4 %psum.169 = f32[4]{0:T(128)S(1)} all-reduce(f32[4]{0:T(128)S(1)} %psum.168), channel_id=1, replica_groups=mesh['slab'=2,'py'=4,'pz'=4] {'slab','py'}, use_global_device_ids=true, to_apply=%region_21.0 | all-reduce | flops 4 | bytes 32 | tf_op jit(solution)/shard_map/psum | solution.py:33
  325.4 8.5 %psum.170 = f32[5]{0:T(128)S(1)} all-reduce(f32[5]{0:T(128)S(1)} %pad_maximum_fusion.137), channel_id=1, replica_groups=mesh['slab'=2,'py'=4,'pz'=4] {'pz'}, use_global_device_ids=true, to_apply=%region_23.0 | all-reduce | flops 5 | bytes 40 | tf_op jit(solution)/shard_map/psum | solution.py:32
  333.9 15.2 %psum.171 = f32[5]{0:T(128)S(1)} all-reduce(f32[5]{0:T(128)S(1)} %psum.170), channel_id=1, replica_groups=mesh['slab'=2,'py'=4,'pz'=4] {'slab','py'}, use_global_device_ids=true, to_apply=%region_24.0 | all-reduce | flops 5 | bytes 40 | tf_op jit(solution)/shard_map/psum | solution.py:33
  361.8 4.0 collective-permute-done.27
  377.6 9.4 %psum.172 = f32[5]{0:T(128)S(1)} all-reduce(f32[5]{0:T(128)S(1)} %fusion.8), channel_id=1, replica_groups=mesh['slab'=2,'py'=4,'pz'=4] {'pz'}, use_global_device_ids=true, to_apply=%region_26.0 | all-reduce | flops 5 | bytes 40 | tf_op jit(solution)/shard_map/psum | solution.py:32
  387.0 14.0 %psum.173 = f32[5]{0:T(128)S(1)} all-reduce(f32[5]{0:T(128)S(1)} %psum.172), channel_id=1, replica_groups=mesh['slab'=2,'py'=4,'pz'=4] {'slab','py'}, use_global_device_ids=true, to_apply=%region_27.0 | all-reduce | flops 5 | bytes 40 | tf_op jit(solution)/shard_map/psum | solution.py:33
  406.8 8.3 %psum.174 = f32[6]{0:T(128)S(1)} all-reduce(f32[6]{0:T(128)S(1)} %pad_maximum_fusion.138), channel_id=1, replica_groups=mesh['slab'=2,'py'=4,'pz'=4] {'pz'}, use_global_device_ids=true, to_apply=%region_29.0 | all-reduce | flops 6 | bytes 48 | tf_op jit(solution)/shard_map/psum | solution.py:32
  416.4 15.6 %psum.175 = f32[6]{0:T(128)S(1)} all-reduce(f32[6]{0:T(128)S(1)} %psum.174), channel_id=1, replica_groups=mesh['slab'=2,'py'=4,'pz'=4] {'slab','py'}, use_global_device_ids=true, to_apply=%region_30.0 | all-reduce | flops 6 | bytes 48 | tf_op jit(solution)/shard_map/psum | solution.py:33
  (142 shorter events, 114.9 us)
Async XLA Ops:
  0.6 30.3 %copy-start.1 = (f32[8,32,128]{2,1,0:T(8,128)S(1)}, f32[8,32,128]{2,1,0:T(8,128)}, u32[]{:S(2)}) copy-start(f32[8,32,128]{2,1,0:T(8,128)} %param.2) | copy-start | bytes 393220
  31.1 5.2 %collective-permute-start = (f32[8,32,1]{2,1,0:T(8,128)S(1)}, f32[8,32,1]{2,1,0:T(8,128)S(1)}, u32[]{:S(2)}, u32[]{:S(2)}) collective-permute-start(f32[8,32,1]{2,1,0:T(8,128)S(1)} %get-tuple-element.52), channel_id=1, source_target_pairs={{0,16},{1,17},{2,18},{3,19},{4,20},{5,21},{6,22},{7,23},{8,24},{9,... | collective-permute-start | bytes 3080 | tf_op jit(solution)/shard_map/ppermute | solution.py:15
  35.0 3.2 collective-permute-start.1
  38.4 2.7 collective-permute-start.2
  39.7 13.6 %copy-start = (f32[8,32,128]{2,1,0:T(8,128)S(1)}, f32[8,32,128]{2,1,0:T(8,128)}, u32[]{:S(2)}) copy-start(f32[8,32,128]{2,1,0:T(8,128)} %param.3) | copy-start | bytes 393220
  39.7 5.7 %collective-permute-start.3 = (f32[8,1,130]{2,1,0:T(1,128)S(1)}, f32[8,1,130]{2,1,0:T(1,128)S(1)}, u32[]{:S(2)}, u32[]{:S(2)}) collective-permute-start(f32[8,1,130]{2,1,0:T(1,128)S(1)} %get-tuple-element.40), channel_id=1, source_target_pairs={{4,0},{8,4},{12,8},{5,1},{9,5},{13,9},{6,2},{10,6},{14,10},{7,3},{... | collective-permute-start | bytes 12488 | tf_op jit(solution)/shard_map/ppermute | solution.py:18
  45.5 3.2 collective-permute-start.5
  47.0 6.3 %collective-permute-start.4 = (f32[1,34,130]{2,1,0:T(8,128)S(1)}, f32[1,34,130]{2,1,0:T(8,128)S(1)}, u32[]{:S(2)}, u32[]{:S(2)}) collective-permute-start(f32[1,34,130]{2,1,0:T(8,128)S(1)} %get-tuple-element.30), channel_id=1, source_target_pairs={{1,0},{2,1},{3,2},{5,4},{6,5},{7,6},{9,8},{10,9},{11,10},{13,12},{... | collective-permute-start | bytes 53048 | tf_op jit(solution)/shard_map/ppermute | solution.py:18
  109.8 3.3 collective-permute-start.6
  111.8 3.2 collective-permute-start.7
  115.2 2.9 collective-permute-start.8
  116.7 5.5 %collective-permute-start.9 = (f32[8,1,130]{2,1,0:T(1,128)S(1)}, f32[8,1,130]{2,1,0:T(1,128)S(1)}, u32[]{:S(2)}, u32[]{:S(2)}) collective-permute-start(f32[8,1,130]{2,1,0:T(1,128)S(1)} %get-tuple-element.38), channel_id=1, source_target_pairs={{4,0},{8,4},{12,8},{5,1},{9,5},{13,9},{6,2},{10,6},{14,10},{7,3},{... | collective-permute-start | bytes 12488 | tf_op jit(solution)/shard_map/ppermute | solution.py:18
  122.4 5.6 %collective-permute-start.11 = (f32[1,34,130]{2,1,0:T(8,128)S(1)}, f32[1,34,130]{2,1,0:T(8,128)S(1)}, u32[]{:S(2)}, u32[]{:S(2)}) collective-permute-start(f32[1,34,130]{2,1,0:T(8,128)S(1)} %get-tuple-element.29), channel_id=1, source_target_pairs={{0,1},{1,2},{2,3},{4,5},{5,6},{6,7},{8,9},{9,10},{10,11},{12,13},{... | collective-permute-start | bytes 53048 | tf_op jit(solution)/shard_map/ppermute | solution.py:15
  126.3 5.9 %collective-permute-start.10 = (f32[1,34,130]{2,1,0:T(8,128)S(1)}, f32[1,34,130]{2,1,0:T(8,128)S(1)}, u32[]{:S(2)}, u32[]{:S(2)}) collective-permute-start(f32[1,34,130]{2,1,0:T(8,128)S(1)} %get-tuple-element.28), channel_id=1, source_target_pairs={{1,0},{2,1},{3,2},{5,4},{6,5},{7,6},{9,8},{10,9},{11,10},{13,12},{... | collective-permute-start | bytes 53048 | tf_op jit(solution)/shard_map/ppermute | solution.py:18
  190.7 3.3 collective-permute-start.12
  192.8 3.2 collective-permute-start.13
  196.1 3.2 collective-permute-start.14
  198.0 5.5 %collective-permute-start.15 = (f32[8,1,130]{2,1,0:T(1,128)S(1)}, f32[8,1,130]{2,1,0:T(1,128)S(1)}, u32[]{:S(2)}, u32[]{:S(2)}) collective-permute-start(f32[8,1,130]{2,1,0:T(1,128)S(1)} %get-tuple-element.36), channel_id=1, source_target_pairs={{4,0},{8,4},{12,8},{5,1},{9,5},{13,9},{6,2},{10,6},{14,10},{7,3},{... | collective-permute-start | bytes 12488 | tf_op jit(solution)/shard_map/ppermute | solution.py:18
  203.7 4.6 %collective-permute-start.17 = (f32[1,34,130]{2,1,0:T(8,128)S(1)}, f32[1,34,130]{2,1,0:T(8,128)S(1)}, u32[]{:S(2)}, u32[]{:S(2)}) collective-permute-start(f32[1,34,130]{2,1,0:T(8,128)S(1)} %get-tuple-element.27), channel_id=1, source_target_pairs={{0,1},{1,2},{2,3},{4,5},{5,6},{6,7},{8,9},{9,10},{10,11},{12,13},{... | collective-permute-start | bytes 53048 | tf_op jit(solution)/shard_map/ppermute | solution.py:15
  206.6 5.9 %collective-permute-start.16 = (f32[1,34,130]{2,1,0:T(8,128)S(1)}, f32[1,34,130]{2,1,0:T(8,128)S(1)}, u32[]{:S(2)}, u32[]{:S(2)}) collective-permute-start(f32[1,34,130]{2,1,0:T(8,128)S(1)} %get-tuple-element.26), channel_id=1, source_target_pairs={{1,0},{2,1},{3,2},{5,4},{6,5},{7,6},{9,8},{10,9},{11,10},{13,12},{... | collective-permute-start | bytes 53048 | tf_op jit(solution)/shard_map/ppermute | solution.py:18
  271.5 3.3 collective-permute-start.18
  273.5 3.2 collective-permute-start.19
  276.9 2.9 collective-permute-start.20
  278.4 5.5 %collective-permute-start.21 = (f32[8,1,130]{2,1,0:T(1,128)S(1)}, f32[8,1,130]{2,1,0:T(1,128)S(1)}, u32[]{:S(2)}, u32[]{:S(2)}) collective-permute-start(f32[8,1,130]{2,1,0:T(1,128)S(1)} %get-tuple-element.34), channel_id=1, source_target_pairs={{4,0},{8,4},{12,8},{5,1},{9,5},{13,9},{6,2},{10,6},{14,10},{7,3},{... | collective-permute-start | bytes 12488 | tf_op jit(solution)/shard_map/ppermute | solution.py:18
  284.1 4.7 %collective-permute-start.23 = (f32[1,34,130]{2,1,0:T(8,128)S(1)}, f32[1,34,130]{2,1,0:T(8,128)S(1)}, u32[]{:S(2)}, u32[]{:S(2)}) collective-permute-start(f32[1,34,130]{2,1,0:T(8,128)S(1)} %get-tuple-element.25), channel_id=1, source_target_pairs={{0,1},{1,2},{2,3},{4,5},{5,6},{6,7},{8,9},{9,10},{10,11},{12,13},{... | collective-permute-start | bytes 53048 | tf_op jit(solution)/shard_map/ppermute | solution.py:15
  287.1 5.9 %collective-permute-start.22 = (f32[1,34,130]{2,1,0:T(8,128)S(1)}, f32[1,34,130]{2,1,0:T(8,128)S(1)}, u32[]{:S(2)}, u32[]{:S(2)}) collective-permute-start(f32[1,34,130]{2,1,0:T(8,128)S(1)} %get-tuple-element.24), channel_id=1, source_target_pairs={{1,0},{2,1},{3,2},{5,4},{6,5},{7,6},{9,8},{10,9},{11,10},{13,12},{... | collective-permute-start | bytes 53048 | tf_op jit(solution)/shard_map/ppermute | solution.py:18
  353.0 5.2 %collective-permute-start.24 = (f32[8,32,1]{2,1,0:T(8,128)S(1)}, f32[8,32,1]{2,1,0:T(8,128)S(1)}, u32[]{:S(2)}, u32[]{:S(2)}) collective-permute-start(f32[8,32,1]{2,1,0:T(8,128)S(1)} %get-tuple-element.43), channel_id=1, source_target_pairs={{0,16},{1,17},{2,18},{3,19},{4,20},{5,21},{6,22},{7,23},{8,24},{9,... | collective-permute-start | bytes 3080 | tf_op jit(solution)/shard_map/ppermute | solution.py:15
  355.0 3.2 collective-permute-start.25
  358.4 3.4 collective-permute-start.26
  360.3 5.5 %collective-permute-start.27 = (f32[8,1,130]{2,1,0:T(1,128)S(1)}, f32[8,1,130]{2,1,0:T(1,128)S(1)}, u32[]{:S(2)}, u32[]{:S(2)}) collective-permute-start(f32[8,1,130]{2,1,0:T(1,128)S(1)} %get-tuple-element.32), channel_id=1, source_target_pairs={{4,0},{8,4},{12,8},{5,1},{9,5},{13,9},{6,2},{10,6},{14,10},{7,3},{... | collective-permute-start | bytes 12488 | tf_op jit(solution)/shard_map/ppermute | solution.py:18
  365.9 6.1 %collective-permute-start.29 = (f32[1,34,130]{2,1,0:T(8,128)S(1)}, f32[1,34,130]{2,1,0:T(8,128)S(1)}, u32[]{:S(2)}, u32[]{:S(2)}) collective-permute-start(f32[1,34,130]{2,1,0:T(8,128)S(1)} %get-tuple-element.23), channel_id=1, source_target_pairs={{0,1},{1,2},{2,3},{4,5},{5,6},{6,7},{8,9},{9,10},{10,11},{12,13},{... | collective-permute-start | bytes 53048 | tf_op jit(solution)/shard_map/ppermute | solution.py:15
  368.8 5.9 %collective-permute-start.28 = (f32[1,34,130]{2,1,0:T(8,128)S(1)}, f32[1,34,130]{2,1,0:T(8,128)S(1)}, u32[]{:S(2)}, u32[]{:S(2)}) collective-permute-start(f32[1,34,130]{2,1,0:T(8,128)S(1)} %get-tuple-element.22), channel_id=1, source_target_pairs={{1,0},{2,1},{3,2},{5,4},{6,5},{7,6},{9,8},{10,9},{11,10},{13,12},{... | collective-permute-start | bytes 53048 | tf_op jit(solution)/shard_map/ppermute | solution.py:18
  (1 other events, 0.9 us)
where the time goes:
time: 440 us; the launch traced here: 439 us
  blocking collectives  266 us (60%)
  starting transfers between devices  54.2 us (12%)
  waiting for transfers between devices  50.1 us (11%)
  matrix products  29.2 us (7%)
  other arithmetic  17.2 us (4%)
  between operations  15.6 us (4%)
  local copies, waits for them, and re-layouts  6.18 us (1%)
    psum x11, blocking collectives, reduce_all(): return lax.psum(inner, ('slab', 'py'))  165 us
    psum x11, blocking collectives, reduce_all(): inner = lax.psum(partials, 'pz')  101 us
    ppermute x15, waiting for transfers between devices, with_halo(): lax.ppermute(lax.slice_in_dim(block, 0, width, axis=dim), axis, backward)  48.7 us
    ppermute x15, starting transfers between devices, with_halo(): lax.ppermute(lax.slice_in_dim(block, block.shape[dim] - width, None, axis...  34.5 us
    ppermute x15, starting transfers between devices, with_halo(): lax.ppermute(lax.slice_in_dim(block, 0, width, axis=dim), axis, backward)  19.7 us
    dot_general x8, matrix products, project(): jnp.einsum('kzyx,zyx->k', active, image, precision=lax.Precision.HIGHEST)  19.6 us
    dot_general x8, matrix products, remove(): jnp.einsum('k,kzyx->zyx', coeffs, active, precision=lax.Precision.HIGHEST)  9.56 us
  transfers between devices with their start and end apart: 30, of which 19 were waited for; matrix products, arithmetic and copies ran while one was open for 0% of the time, Pallas kernels for 0%

commit v1 on v0

--- a/solution.py
+++ b/solution.py
@@ -30,7 +30,7 @@
 
 def reduce_all(partials):
     inner = lax.psum(partials, "pz")
-    return lax.psum(inner, ("slab", "py"))
+    return lax.psum(lax.psum(inner, "py"), "slab")
 
 
 def project(active, image):

time: 440 us -> 413 us (0.939)
  blocking collectives: 266 us -> 237 us
    psum x11 -> x22, blocking collectives: 165 us -> 135 us  [reduce_all(): return lax.psum(lax.psum(inner, 'py'), 'slab')]
  transfers between devices with their start and end apart: 30 -> 30, of which waited for: 19 -> 20; matrix products, arithmetic and copies ran while one was open for 0% -> 0% of each run, Pallas kernels for 0% -> 0%
where the time goes in v1:
time: 413 us; the launch traced here: 411 us
  blocking collectives  237 us (57%)
  starting transfers between devices  54 us (13%)
  waiting for transfers between devices  52.2 us (13%)
  matrix products  29.2 us (7%)
  other arithmetic  17.2 us (4%)
  between operations  15.6 us (4%)
  local copies, waits for them, and re-layouts  6.18 us (1%)
    psum x22, blocking collectives, reduce_all(): return lax.psum(lax.psum(inner, 'py'), 'slab')  135 us
    psum x11, blocking collectives, reduce_all(): inner = lax.psum(partials, 'pz')  101 us
    ppermute x15, waiting for transfers between devices, with_halo(): lax.ppermute(lax.slice_in_dim(block, 0, width, axis=dim), axis, backward)  50.4 us
    ppermute x15, starting transfers between devices, with_halo(): lax.ppermute(lax.slice_in_dim(block, block.shape[dim] - width, None, axis...  34.5 us
    dot_general x8, matrix products, project(): jnp.einsum('kzyx,zyx->k', active, image, precision=lax.Precision.HIGHEST)  19.6 us
    ppermute x15, starting transfers between devices, with_halo(): lax.ppermute(lax.slice_in_dim(block, 0, width, axis=dim), axis, backward)  19.5 us
    dot_general x8, matrix products, remove(): jnp.einsum('k,kzyx->zyx', coeffs, active, precision=lax.Precision.HIGHEST)  9.57 us
  transfers between devices with their start and end apart: 30, of which 20 were waited for; matrix products, arithmetic and copies ran while one was open for 0% of the time, Pallas kernels for 0%

profile of v1, /device:TPU:0, one launch (start us, length us, event | category | flops | bytes accessed | tf_op | source)
XLA Modules:
  0.0 411.0 jit_solution(12547723713136495679)
XLA Ops:
  2.2 12.0 %psum.231 = f32[1]{0:T(128)} all-reduce(f32[1]{0:T(128)} %bitcast.4), channel_id=1, replica_groups=mesh['slab'=2,'py'=4,'pz'=4] {'pz'}, use_global_device_ids=true, to_apply=%region_1.0 | all-reduce | flops 1 | bytes 8 | tf_op jit(solution)/shard_map/psum | solution.py:32
  14.2 12.6 %psum.232 = f32[1]{0:T(128)} all-reduce(f32[1]{0:T(128)} %psum.231), channel_id=1, replica_groups=mesh['slab'=2,'py'=4,'pz'=4] {'py'}, use_global_device_ids=true, to_apply=%region_2.0 | all-reduce | flops 1 | bytes 8 | tf_op jit(solution)/shard_map/psum | solution.py:33
  38.9 4.2 %collective-permute-done.3 = f32[8,1,130]{2,1,0:T(1,128)S(1)} collective-permute-done((f32[8,1,130]{2,1,0:T(1,128)S(1)}, f32[8,1,130]{2,1,0:T(1,128)S(1)}, u32[]{:S(2)}, u32[]{:S(2)}) %collective-permute-start.3) | collective-permute-done | bytes 4192 | tf_op jit(solution)/shard_map/ppermute | solution.py:18
  46.5 4.6 %collective-permute-done.4 = f32[1,34,130]{2,1,0:T(8,128)S(1)} collective-permute-done((f32[1,34,130]{2,1,0:T(8,128)S(1)}, f32[1,34,130]{2,1,0:T(8,128)S(1)}, u32[]{:S(2)}, u32[]{:S(2)}) %collective-permute-start.4) | collective-permute-done | bytes 17712 | tf_op jit(solution)/shard_map/ppermute | solution.py:18
  52.0 11.0 %psum.234 = f32[1]{0:T(128)} all-reduce(f32[1]{0:T(128)} %bitcast.7), channel_id=1, replica_groups=mesh['slab'=2,'py'=4,'pz'=4] {'pz'}, use_global_device_ids=true, to_apply=%region_4.0 | all-reduce | flops 1 | bytes 8 | tf_op jit(solution)/shard_map/psum | solution.py:32
  63.0 9.8 %psum.235 = f32[1]{0:T(128)} all-reduce(f32[1]{0:T(128)} %psum.234), channel_id=1, replica_groups=mesh['slab'=2,'py'=4,'pz'=4] {'py'}, use_global_device_ids=true, to_apply=%region_5.0 | all-reduce | flops 1 | bytes 8 | tf_op jit(solution)/shard_map/psum | solution.py:33
  79.3 7.4 %psum.237 = f32[2]{0:T(128)S(1)} all-reduce(f32[2]{0:T(128)S(1)} %pad_maximum_fusion.134), channel_id=1, replica_groups=mesh['slab'=2,'py'=4,'pz'=4] {'pz'}, use_global_device_ids=true, to_apply=%region_8.0 | all-reduce | flops 2 | bytes 16 | tf_op jit(solution)/shard_map/psum | solution.py:32
  86.7 9.6 %psum.238 = f32[2]{0:T(128)S(1)} all-reduce(f32[2]{0:T(128)S(1)} %psum.237), channel_id=1, replica_groups=mesh['slab'=2,'py'=4,'pz'=4] {'py'}, use_global_device_ids=true, to_apply=%region_9.0 | all-reduce | flops 2 | bytes 16 | tf_op jit(solution)/shard_map/psum | solution.py:33
  111.7 4.2 %collective-permute-done.9 = f32[8,1,130]{2,1,0:T(1,128)S(1)} collective-permute-done((f32[8,1,130]{2,1,0:T(1,128)S(1)}, f32[8,1,130]{2,1,0:T(1,128)S(1)}, u32[]{:S(2)}, u32[]{:S(2)}) %collective-permute-start.9) | collective-permute-done | bytes 4192 | tf_op jit(solution)/shard_map/ppermute | solution.py:18
  121.6 4.2 %collective-permute-done.10 = f32[1,34,130]{2,1,0:T(8,128)S(1)} collective-permute-done((f32[1,34,130]{2,1,0:T(8,128)S(1)}, f32[1,34,130]{2,1,0:T(8,128)S(1)}, u32[]{:S(2)}, u32[]{:S(2)}) %collective-permute-start.10) | collective-permute-done | bytes 17712 | tf_op jit(solution)/shard_map/ppermute | solution.py:18
  128.6 9.3 %psum.240 = f32[2]{0:T(128)S(1)} all-reduce(f32[2]{0:T(128)S(1)} %convolution_bitcast_fusion.5), channel_id=1, replica_groups=mesh['slab'=2,'py'=4,'pz'=4] {'pz'}, use_global_device_ids=true, to_apply=%region_11.0 | all-reduce | flops 2 | bytes 16 | tf_op jit(solution)/shard_map/psum | solution.py:32
  137.8 8.4 %psum.241 = f32[2]{0:T(128)S(1)} all-reduce(f32[2]{0:T(128)S(1)} %psum.240), channel_id=1, replica_groups=mesh['slab'=2,'py'=4,'pz'=4] {'py'}, use_global_device_ids=true, to_apply=%region_12.0 | all-reduce | flops 2 | bytes 16 | tf_op jit(solution)/shard_map/psum | solution.py:33
  153.4 8.5 %psum.243 = f32[3]{0:T(128)S(1)} all-reduce(f32[3]{0:T(128)S(1)} %pad_maximum_fusion.135), channel_id=1, replica_groups=mesh['slab'=2,'py'=4,'pz'=4] {'pz'}, use_global_device_ids=true, to_apply=%region_15.0 | all-reduce | flops 3 | bytes 24 | tf_op jit(solution)/shard_map/psum | solution.py:32
  161.9 10.3 %psum.244 = f32[3]{0:T(128)S(1)} all-reduce(f32[3]{0:T(128)S(1)} %psum.243), channel_id=1, replica_groups=mesh['slab'=2,'py'=4,'pz'=4] {'py'}, use_global_device_ids=true, to_apply=%region_16.0 | all-reduce | flops 3 | bytes 24 | tf_op jit(solution)/shard_map/psum | solution.py:33
  187.1 4.2 %collective-permute-done.15 = f32[8,1,130]{2,1,0:T(1,128)S(1)} collective-permute-done((f32[8,1,130]{2,1,0:T(1,128)S(1)}, f32[8,1,130]{2,1,0:T(1,128)S(1)}, u32[]{:S(2)}, u32[]{:S(2)}) %collective-permute-start.15) | collective-permute-done | bytes 4192 | tf_op jit(solution)/shard_map/ppermute | solution.py:18
  195.9 4.2 %collective-permute-done.16 = f32[1,34,130]{2,1,0:T(8,128)S(1)} collective-permute-done((f32[1,34,130]{2,1,0:T(8,128)S(1)}, f32[1,34,130]{2,1,0:T(8,128)S(1)}, u32[]{:S(2)}, u32[]{:S(2)}) %collective-permute-start.16) | collective-permute-done | bytes 17712 | tf_op jit(solution)/shard_map/ppermute | solution.py:18
  202.9 9.4 %psum.246 = f32[3]{0:T(128)S(1)} all-reduce(f32[3]{0:T(128)S(1)} %convolution_bitcast_fusion.3), channel_id=1, replica_groups=mesh['slab'=2,'py'=4,'pz'=4] {'pz'}, use_global_device_ids=true, to_apply=%region_19.0 | all-reduce | flops 3 | bytes 24 | tf_op jit(solution)/shard_map/psum | solution.py:32
  212.3 8.7 %psum.247 = f32[3]{0:T(128)S(1)} all-reduce(f32[3]{0:T(128)S(1)} %psum.246), channel_id=1, replica_groups=mesh['slab'=2,'py'=4,'pz'=4] {'py'}, use_global_device_ids=true, to_apply=%region_20.0 | all-reduce | flops 3 | bytes 24 | tf_op jit(solution)/shard_map/psum | solution.py:33
  228.4 8.3 %psum.249 = f32[4]{0:T(128)S(1)} all-reduce(f32[4]{0:T(128)S(1)} %pad_maximum_fusion.136), channel_id=1, replica_groups=mesh['slab'=2,'py'=4,'pz'=4] {'pz'}, use_global_device_ids=true, to_apply=%region_23.0 | all-reduce | flops 4 | bytes 32 | tf_op jit(solution)/shard_map/psum | solution.py:32
  236.7 10.2 %psum.250 = f32[4]{0:T(128)S(1)} all-reduce(f32[4]{0:T(128)S(1)} %psum.249), channel_id=1, replica_groups=mesh['slab'=2,'py'=4,'pz'=4] {'py'}, use_global_device_ids=true, to_apply=%region_24.0 | all-reduce | flops 4 | bytes 32 | tf_op jit(solution)/shard_map/psum | solution.py:33
  262.1 4.2 %collective-permute-done.21 = f32[8,1,130]{2,1,0:T(1,128)S(1)} collective-permute-done((f32[8,1,130]{2,1,0:T(1,128)S(1)}, f32[8,1,130]{2,1,0:T(1,128)S(1)}, u32[]{:S(2)}, u32[]{:S(2)}) %collective-permute-start.21) | collective-permute-done | bytes 4192 | tf_op jit(solution)/shard_map/ppermute | solution.py:18
  271.1 4.2 %collective-permute-done.22 = f32[1,34,130]{2,1,0:T(8,128)S(1)} collective-permute-done((f32[1,34,130]{2,1,0:T(8,128)S(1)}, f32[1,34,130]{2,1,0:T(8,128)S(1)}, u32[]{:S(2)}, u32[]{:S(2)}) %collective-permute-start.22) | collective-permute-done | bytes 17712 | tf_op jit(solution)/shard_map/ppermute | solution.py:18
  278.3 9.3 %psum.252 = f32[4]{0:T(128)S(1)} all-reduce(f32[4]{0:T(128)S(1)} %convolution_bitcast_fusion.1), channel_id=1, replica_groups=mesh['slab'=2,'py'=4,'pz'=4] {'pz'}, use_global_device_ids=true, to_apply=%region_27.0 | all-reduce | flops 4 | bytes 32 | tf_op jit(solution)/shard_map/psum | solution.py:32
  287.5 8.4 %psum.253 = f32[4]{0:T(128)S(1)} all-reduce(f32[4]{0:T(128)S(1)} %psum.252), channel_id=1, replica_groups=mesh['slab'=2,'py'=4,'pz'=4] {'py'}, use_global_device_ids=true, to_apply=%region_28.0 | all-reduce | flops 4 | bytes 32 | tf_op jit(solution)/shard_map/psum | solution.py:33
  303.5 8.5 %psum.255 = f32[5]{0:T(128)S(1)} all-reduce(f32[5]{0:T(128)S(1)} %pad_maximum_fusion.137), channel_id=1, replica_groups=mesh['slab'=2,'py'=4,'pz'=4] {'pz'}, use_global_device_ids=true, to_apply=%region_31.0 | all-reduce | flops 5 | bytes 40 | tf_op jit(solution)/shard_map/psum | solution.py:32
  312.7 10.4 %psum.256 = f32[5]{0:T(128)S(1)} all-reduce(f32[5]{0:T(128)S(1)} %psum.255), channel_id=1, replica_groups=mesh['slab'=2,'py'=4,'pz'=4] {'py'}, use_global_device_ids=true, to_apply=%region_32.0 | all-reduce | flops 5 | bytes 40 | tf_op jit(solution)/shard_map/psum | solution.py:33
  338.0 4.2 %collective-permute-done.27 = f32[8,1,130]{2,1,0:T(1,128)S(1)} collective-permute-done((f32[8,1,130]{2,1,0:T(1,128)S(1)}, f32[8,1,130]{2,1,0:T(1,128)S(1)}, u32[]{:S(2)}, u32[]{:S(2)}) %collective-permute-start.27) | collective-permute-done | bytes 4192 | tf_op jit(solution)/shard_map/ppermute | solution.py:18
  346.9 4.2 %collective-permute-done.28 = f32[1,34,130]{2,1,0:T(8,128)S(1)} collective-permute-done((f32[1,34,130]{2,1,0:T(8,128)S(1)}, f32[1,34,130]{2,1,0:T(8,128)S(1)}, u32[]{:S(2)}, u32[]{:S(2)}) %collective-permute-start.28) | collective-permute-done | bytes 17712 | tf_op jit(solution)/shard_map/ppermute | solution.py:18
  354.6 9.4 %psum.258 = f32[5]{0:T(128)S(1)} all-reduce(f32[5]{0:T(128)S(1)} %fusion.8), channel_id=1, replica_groups=mesh['slab'=2,'py'=4,'pz'=4] {'pz'}, use_global_device_ids=true, to_apply=%region_35.0 | all-reduce | flops 5 | bytes 40 | tf_op jit(solution)/shard_map/psum | solution.py:32
  365.2 8.6 %psum.259 = f32[5]{0:T(128)S(1)} all-reduce(f32[5]{0:T(128)S(1)} %psum.258), channel_id=1, replica_groups=mesh['slab'=2,'py'=4,'pz'=4] {'py'}, use_global_device_ids=true, to_apply=%region_36.0 | all-reduce | flops 5 | bytes 40 | tf_op jit(solution)/shard_map/psum | solution.py:33
  381.5 8.3 %psum.261 = f32[6]{0:T(128)S(1)} all-reduce(f32[6]{0:T(128)S(1)} %pad_maximum_fusion.138), channel_id=1, replica_groups=mesh['slab'=2,'py'=4,'pz'=4] {'pz'}, use_global_device_ids=true, to_apply=%region_39.0 | all-reduce | flops 6 | bytes 48 | tf_op jit(solution)/shard_map/psum | solution.py:32
  390.4 10.1 %psum.262 = f32[6]{0:T(128)S(1)} all-reduce(f32[6]{0:T(128)S(1)} %psum.261), channel_id=1, replica_groups=mesh['slab'=2,'py'=4,'pz'=4] {'py'}, use_global_device_ids=true, to_apply=%region_40.0 | all-reduce | flops 6 | bytes 48 | tf_op jit(solution)/shard_map/psum | solution.py:33
  (153 shorter events, 144.5 us)
Async XLA Ops:
  0.6 29.9 %copy-start.1 = (f32[8,32,128]{2,1,0:T(8,128)S(1)}, f32[8,32,128]{2,1,0:T(8,128)}, u32[]{:S(2)}) copy-start(f32[8,32,128]{2,1,0:T(8,128)} %param.2) | copy-start | bytes 393220
  30.7 3.4 collective-permute-start
  32.8 3.2 collective-permute-start.1
  36.2 2.7 collective-permute-start.2
  37.5 13.6 %copy-start = (f32[8,32,128]{2,1,0:T(8,128)S(1)}, f32[8,32,128]{2,1,0:T(8,128)}, u32[]{:S(2)}) copy-start(f32[8,32,128]{2,1,0:T(8,128)} %param.3) | copy-start | bytes 393220
  37.5 5.7 %collective-permute-start.3 = (f32[8,1,130]{2,1,0:T(1,128)S(1)}, f32[8,1,130]{2,1,0:T(1,128)S(1)}, u32[]{:S(2)}, u32[]{:S(2)}) collective-permute-start(f32[8,1,130]{2,1,0:T(1,128)S(1)} %get-tuple-element.40), channel_id=1, source_target_pairs={{4,0},{8,4},{12,8},{5,1},{9,5},{13,9},{6,2},{10,6},{14,10},{7,3},{... | collective-permute-start | bytes 12488 | tf_op jit(solution)/shard_map/ppermute | solution.py:18
  43.3 3.2 collective-permute-start.5
  44.8 6.3 %collective-permute-start.4 = (f32[1,34,130]{2,1,0:T(8,128)S(1)}, f32[1,34,130]{2,1,0:T(8,128)S(1)}, u32[]{:S(2)}, u32[]{:S(2)}) collective-permute-start(f32[1,34,130]{2,1,0:T(8,128)S(1)} %get-tuple-element.30), channel_id=1, source_target_pairs={{1,0},{2,1},{3,2},{5,4},{6,5},{7,6},{9,8},{10,9},{11,10},{13,12},{... | collective-permute-start | bytes 53048 | tf_op jit(solution)/shard_map/ppermute | solution.py:18
  102.2 3.4 collective-permute-start.6
  104.3 3.2 collective-permute-start.7
  107.7 4.0 collective-permute-start.8
  110.3 5.5 %collective-permute-start.9 = (f32[8,1,130]{2,1,0:T(1,128)S(1)}, f32[8,1,130]{2,1,0:T(1,128)S(1)}, u32[]{:S(2)}, u32[]{:S(2)}) collective-permute-start(f32[8,1,130]{2,1,0:T(1,128)S(1)} %get-tuple-element.38), channel_id=1, source_target_pairs={{4,0},{8,4},{12,8},{5,1},{9,5},{13,9},{6,2},{10,6},{14,10},{7,3},{... | collective-permute-start | bytes 12488 | tf_op jit(solution)/shard_map/ppermute | solution.py:18
  116.0 5.6 %collective-permute-start.11 = (f32[1,34,130]{2,1,0:T(8,128)S(1)}, f32[1,34,130]{2,1,0:T(8,128)S(1)}, u32[]{:S(2)}, u32[]{:S(2)}) collective-permute-start(f32[1,34,130]{2,1,0:T(8,128)S(1)} %get-tuple-element.29), channel_id=1, source_target_pairs={{0,1},{1,2},{2,3},{4,5},{5,6},{6,7},{8,9},{9,10},{10,11},{12,13},{... | collective-permute-start | bytes 53048 | tf_op jit(solution)/shard_map/ppermute | solution.py:15
  119.9 5.9 %collective-permute-start.10 = (f32[1,34,130]{2,1,0:T(8,128)S(1)}, f32[1,34,130]{2,1,0:T(8,128)S(1)}, u32[]{:S(2)}, u32[]{:S(2)}) collective-permute-start(f32[1,34,130]{2,1,0:T(8,128)S(1)} %get-tuple-element.28), channel_id=1, source_target_pairs={{1,0},{2,1},{3,2},{5,4},{6,5},{7,6},{9,8},{10,9},{11,10},{13,12},{... | collective-permute-start | bytes 53048 | tf_op jit(solution)/shard_map/ppermute | solution.py:18
  178.4 3.4 collective-permute-start.12
  180.5 3.2 collective-permute-start.13
  183.8 3.2 collective-permute-start.14
  185.7 5.5 %collective-permute-start.15 = (f32[8,1,130]{2,1,0:T(1,128)S(1)}, f32[8,1,130]{2,1,0:T(1,128)S(1)}, u32[]{:S(2)}, u32[]{:S(2)}) collective-permute-start(f32[8,1,130]{2,1,0:T(1,128)S(1)} %get-tuple-element.36), channel_id=1, source_target_pairs={{4,0},{8,4},{12,8},{5,1},{9,5},{13,9},{6,2},{10,6},{14,10},{7,3},{... | collective-permute-start | bytes 12488 | tf_op jit(solution)/shard_map/ppermute | solution.py:18
  191.4 4.6 %collective-permute-start.17 = (f32[1,34,130]{2,1,0:T(8,128)S(1)}, f32[1,34,130]{2,1,0:T(8,128)S(1)}, u32[]{:S(2)}, u32[]{:S(2)}) collective-permute-start(f32[1,34,130]{2,1,0:T(8,128)S(1)} %get-tuple-element.27), channel_id=1, source_target_pairs={{0,1},{1,2},{2,3},{4,5},{5,6},{6,7},{8,9},{9,10},{10,11},{12,13},{... | collective-permute-start | bytes 53048 | tf_op jit(solution)/shard_map/ppermute | solution.py:15
  194.3 5.9 %collective-permute-start.16 = (f32[1,34,130]{2,1,0:T(8,128)S(1)}, f32[1,34,130]{2,1,0:T(8,128)S(1)}, u32[]{:S(2)}, u32[]{:S(2)}) collective-permute-start(f32[1,34,130]{2,1,0:T(8,128)S(1)} %get-tuple-element.26), channel_id=1, source_target_pairs={{1,0},{2,1},{3,2},{5,4},{6,5},{7,6},{9,8},{10,9},{11,10},{13,12},{... | collective-permute-start | bytes 53048 | tf_op jit(solution)/shard_map/ppermute | solution.py:18
  253.2 3.4 collective-permute-start.18
  255.3 3.2 collective-permute-start.19
  258.6 3.4 collective-permute-start.20
  260.7 5.5 %collective-permute-start.21 = (f32[8,1,130]{2,1,0:T(1,128)S(1)}, f32[8,1,130]{2,1,0:T(1,128)S(1)}, u32[]{:S(2)}, u32[]{:S(2)}) collective-permute-start(f32[8,1,130]{2,1,0:T(1,128)S(1)} %get-tuple-element.34), channel_id=1, source_target_pairs={{4,0},{8,4},{12,8},{5,1},{9,5},{13,9},{6,2},{10,6},{14,10},{7,3},{... | collective-permute-start | bytes 12488 | tf_op jit(solution)/shard_map/ppermute | solution.py:18
  266.4 4.7 %collective-permute-start.23 = (f32[1,34,130]{2,1,0:T(8,128)S(1)}, f32[1,34,130]{2,1,0:T(8,128)S(1)}, u32[]{:S(2)}, u32[]{:S(2)}) collective-permute-start(f32[1,34,130]{2,1,0:T(8,128)S(1)} %get-tuple-element.25), channel_id=1, source_target_pairs={{0,1},{1,2},{2,3},{4,5},{5,6},{6,7},{8,9},{9,10},{10,11},{12,13},{... | collective-permute-start | bytes 53048 | tf_op jit(solution)/shard_map/ppermute | solution.py:15
  269.5 5.9 %collective-permute-start.22 = (f32[1,34,130]{2,1,0:T(8,128)S(1)}, f32[1,34,130]{2,1,0:T(8,128)S(1)}, u32[]{:S(2)}, u32[]{:S(2)}) collective-permute-start(f32[1,34,130]{2,1,0:T(8,128)S(1)} %get-tuple-element.24), channel_id=1, source_target_pairs={{1,0},{2,1},{3,2},{5,4},{6,5},{7,6},{9,8},{10,9},{11,10},{13,12},{... | collective-permute-start | bytes 53048 | tf_op jit(solution)/shard_map/ppermute | solution.py:18
  329.3 5.3 %collective-permute-start.24 = (f32[8,32,1]{2,1,0:T(8,128)S(1)}, f32[8,32,1]{2,1,0:T(8,128)S(1)}, u32[]{:S(2)}, u32[]{:S(2)}) collective-permute-start(f32[8,32,1]{2,1,0:T(8,128)S(1)} %get-tuple-element.43), channel_id=1, source_target_pairs={{0,16},{1,17},{2,18},{3,19},{4,20},{5,21},{6,22},{7,23},{8,24},{9,... | collective-permute-start | bytes 3080 | tf_op jit(solution)/shard_map/ppermute | solution.py:15
  331.4 3.2 collective-permute-start.25
  334.8 3.2 collective-permute-start.26
  336.7 5.5 %collective-permute-start.27 = (f32[8,1,130]{2,1,0:T(1,128)S(1)}, f32[8,1,130]{2,1,0:T(1,128)S(1)}, u32[]{:S(2)}, u32[]{:S(2)}) collective-permute-start(f32[8,1,130]{2,1,0:T(1,128)S(1)} %get-tuple-element.32), channel_id=1, source_target_pairs={{4,0},{8,4},{12,8},{5,1},{9,5},{13,9},{6,2},{10,6},{14,10},{7,3},{... | collective-permute-start | bytes 12488 | tf_op jit(solution)/shard_map/ppermute | solution.py:18
  342.3 4.6 %collective-permute-start.29 = (f32[1,34,130]{2,1,0:T(8,128)S(1)}, f32[1,34,130]{2,1,0:T(8,128)S(1)}, u32[]{:S(2)}, u32[]{:S(2)}) collective-permute-start(f32[1,34,130]{2,1,0:T(8,128)S(1)} %get-tuple-element.23), channel_id=1, source_target_pairs={{0,1},{1,2},{2,3},{4,5},{5,6},{6,7},{8,9},{9,10},{10,11},{12,13},{... | collective-permute-start | bytes 53048 | tf_op jit(solution)/shard_map/ppermute | solution.py:15
  345.2 5.9 %collective-permute-start.28 = (f32[1,34,130]{2,1,0:T(8,128)S(1)}, f32[1,34,130]{2,1,0:T(8,128)S(1)}, u32[]{:S(2)}, u32[]{:S(2)}) collective-permute-start(f32[1,34,130]{2,1,0:T(8,128)S(1)} %get-tuple-element.22), channel_id=1, source_target_pairs={{1,0},{2,1},{3,2},{5,4},{6,5},{7,6},{9,8},{10,9},{11,10},{13,12},{... | collective-permute-start | bytes 53048 | tf_op jit(solution)/shard_map/ppermute | solution.py:18
  (1 other events, 0.9 us)
